TPU v7x, 32 devices: a whole 2x2x4 slice. The times are simulated.
32 devices in a mesh: row: 4 (over y, x), col: 8 (over z, core).
Axes of the slice: x: 2, y: 2, z: 4, core: 2. Of those that a mesh axis runs over, the one named last changes fastest.
Arguments:
- values: bfloat16 [4096, 4096], P('row', 'col'), may hold values from 0.0001296997 to 0.12988281
- tile_mask: int32 [32, 32], P('row', 'col'), may hold values 0 or 1
- keep_mask: int32 [32, 32], P('row', 'col'), may hold values 0 or 1
- thr_index: int32 [4096], P('col'), may hold values from 0 to 9
Outputs:
- expanded: bfloat16 [4096, 4096], P('row', 'col')
All inputs are finite; a program needn't handle non-finite values. No bound on the sum of `tile_mask` or of `keep_mask` on one device may be relied on, other than what follows from the above.
Results may differ from a plain program's by a relative error of at most 0.0004.
Values may be sent and summed in bfloat16 or wider, within the bound.
No kernel may reach another device: no remote copies, remote signals or barrier semaphores. Data moves between devices by JAX's collectives and lax.ppermute only.
A program may use at most 64 MiB of HBM per device.

v0:
```python
import jax
import jax.numpy as jnp
from jax import lax
from jax.sharding import PartitionSpec as P

TB = 128


def on_device(values, tile_mask, keep_mask, thr_index):
    row_count, col_count = values.shape
    row_tiles = row_count // TB
    col_tiles = col_count // TB
    matrix = (
        values.reshape(row_tiles, TB, col_tiles, TB)
        * tile_mask[:, None, :, None].astype(jnp.bfloat16)
    ).reshape(row_count, col_count)
    kept_cells = jnp.broadcast_to(
        keep_mask[:, None, :, None].astype(jnp.float32), (row_tiles, TB, col_tiles, TB)
    ).reshape(row_count, col_count)
    order_all = row_count * lax.axis_size("row")
    thresholds = 0.125 * thr_index.astype(jnp.float32)
    col_panel = lax.all_gather(matrix, "row", axis=0, tiled=True)
    product = jnp.dot(
        lax.all_gather(matrix, "col", axis=1, tiled=True),
        col_panel,
        preferred_element_type=jnp.float32,
    )
    outputs = []
    for phase_idx in range(col_tiles):
        lo_col = phase_idx * TB
        part_prod = product[:, lo_col : lo_col + TB]
        col_means = lax.psum(jnp.sum(part_prod, axis=0), "row") / order_all
        pruned = (
            jnp.maximum(part_prod - thresholds[lo_col : lo_col + TB] * col_means, 0.0)
            * kept_cells[:, lo_col : lo_col + TB]
        )
        col_totals = lax.psum(jnp.sum(pruned, axis=0), "row") / order_all
        outputs.append(pruned / jnp.maximum(col_totals, 0.1))
    result = jnp.concatenate(outputs, axis=1)
    return result.astype(jnp.bfloat16)


def solution(mesh):
    return jax.shard_map(
        on_device,
        mesh=mesh,
        in_specs=(P("row", "col"), P("row", "col"), P("row", "col"), P("col")),
        out_specs=P("row", "col"),
        check_vma=False,
    )
```

profile of v0, /device:TPU:0, one launch (start us, length us, event | category | flops | bytes accessed | tf_op | source)
XLA Modules:
  0.0 188.3 jit_solution(8773886451617511830)
XLA Ops:
  6.5 0.0 all-gather.5.cloned.1.call-start
  6.5 0.7 convert_element_type.12
  7.2 0.1 copy.5
  7.3 0.3 mul.41
  7.7 0.0 copy-start.1
  7.7 2.3 %bitcast_multiply_fusion = bf16[1024,512]{1,0:T(8,128)(2,1)} fusion(bf16[1024,512]{1,0:T(8,128)(2,1)} %param.4, bf16[128,8,4,128]{3,2,1,0:T(4,128)(2,1)S(1)} %bitcast.14), kind=kLoop, calls=%fused_computation.1 | loop fusion | flops 524288 | bytes 3145728 | tf_op jit(solution)/shard_map/mul | solution.py:14
  10.0 0.0 all-gather.5.cloned.1.call-update
  10.0 0.0 all-gather.3.cloned.1.call-start
  10.1 0.7 all-gather.3.cloned.1.call-update
  10.8 0.0 copy-done.1
  10.8 0.1 copy.6
  10.9 0.3 broadcast_in_dim.2
  11.2 0.0 copy-start.2
  11.3 0.2 copy.11
  11.4 0.5 copy-done.2
  11.9 53.6 %all-gather.5.cloned.1.call-done = bf16[4096,512]{1,0:T(8,128)(2,1)} async-done(((bf16[1024,512]{1,0:T(8,128)(2,1)}), bf16[4096,512]{1,0:T(8,128)(2,1)}) %all-gather.5.cloned.1.call-update) | async-done | bytes 4194320 | tf_op jit(solution)/shard_map/all_gather | solution.py:22
  65.5 83.7 %all-gather.3.cloned.1.call-done = bf16[1024,4096]{1,0:T(8,128)(2,1)} async-done(((bf16[1024,512]{1,0:T(8,128)(2,1)}), bf16[1024,4096]{1,0:T(8,128)(2,1)}) %all-gather.3.cloned.1.call-update) | async-done | bytes 8388624 | tf_op jit(solution)/shard_map/all_gather | solution.py:24
  149.2 8.1 %fusion.4 = f32[1024,512]{1,0:T(8,128)S(1)} fusion(bf16[1024,4096]{1,0:T(8,128)(2,1)} %all-gather.3.cloned.1.call-done, bf16[4096,512]{1,0:T(8,128)(2,1)} %all-gather.5.cloned.1.call-done), kind=kOutput, calls=%fused_computation.28 | convolution fusion | flops 4294967296 | bytes 14680064 | tf_op jit(solution)/shard_map/dot_general | solution.py:23
  157.3 0.0 copy-start
  157.3 1.3 copy-done
  158.7 0.2 slice_reduce_fusion.3
  158.8 9.8 %all-reduce.1 = (f32[128]{0:T(128)S(1)}, f32[128]{0:T(128)S(1)}, f32[128]{0:T(128)S(1)}, f32[128]{0:T(128)S(1)}) all-reduce(f32[128]{0:T(128)S(1)} %get-tuple-element.9, f32[128]{0:T(128)S(1)} %get-tuple-element.10, f32[128]{0:T(128)S(1)} %get-tuple-element.11, f32[128]{0:T(128)S(1)} %get-tuple-element.12), channel_id=1, replica_groups=mesh['row'=4,'col'=8] {'row'}, use_global_device_ids=true, to_apply=%region_1.0 | all-reduce | flops 512 | bytes 4096 | tf_op jit(solution)/shard_map/psum | solution.py:32
  168.7 1.8 fusion
  170.5 8.0 %all-reduce = (f32[128]{0:T(128)S(1)}, f32[128]{0:T(128)S(1)}, f32[128]{0:T(128)S(1)}, f32[128]{0:T(128)S(1)}) all-reduce(f32[128]{0:T(128)S(1)} %get-tuple-element.6, f32[128]{0:T(128)S(1)} %get-tuple-element.7, f32[128]{0:T(128)S(1)} %get-tuple-element.8, f32[128]{0:T(128)S(1)} %get-tuple-element.5), channel_id=1, replica_groups=mesh['row'=4,'col'=8] {'row'}, use_global_device_ids=true, to_apply=%region_15.0 | all-reduce | flops 512 | bytes 4096 | tf_op jit(solution)/shard_map/psum | solution.py:37
  178.5 1.9 %divide_convert_fusion.3 = (bf16[1024,128]{1,0:T(8,128)(2,1)S(1)}, bf16[1024,128]{1,0:T(8,128)(2,1)S(1)}, bf16[1024,128]{1,0:T(8,128)(2,1)S(1)}, bf16[1024,128]{1,0:T(8,128)(2,1)S(1)}) fusion(f32[128]{0:T(128)S(1)} %get-tuple-element.32, f32[1024,512]{1,0:T(8,128)S(1)} %bitcast.12, f32[128]{0:T(128)S(1)} %get-tuple-element.28, f32[1024,512]{1,0:T(8,128)} %copy-done, ...), kind=kLoop, calls=%fused_computation.10 | loop fusion | flops 2621440 | bytes 5246976 | tf_op jit(solution)/shard_map/convert
  180.4 1.1 pad_maximum_fusion
  (5 shorter events, 0.0 us)
Async XLA Ops:
  6.5 59.0 %all-gather.5.cloned.1.call-start = ((), (), s32[]{:S(2)}) async-start(), calls=%async_computation.1 | async-start | bytes 5242880 | tf_op jit(solution)/shard_map/all_gather | solution.py:22
  7.7 3.1 %copy-start.1 = (s32[8,4]{0,1:T(4,128)S(1)}, s32[8,4]{0,1:T(4,128)}, u32[]{:S(2)}) copy-start(s32[8,4]{0,1:T(4,128)} %param.6) | copy-start | bytes 388
  10.0 139.1 %all-gather.3.cloned.1.call-start = ((), (), s32[]{:S(2)}) async-start(), calls=%async_computation | async-start | bytes 9437184 | tf_op jit(solution)/shard_map/all_gather | solution.py:24
  11.2 0.7 copy-start.2
  157.3 1.4 copy-start
Sparse Core Ops, SparseCore 0:
  10.2 55.2 all-gather.4
  67.1 82.0 all-gather.2
where the time goes:
time: 189 us; the launch traced here: 188 us
  waiting for transfers between devices  138 us (73%)
  blocking collectives  17.8 us (9%)
  between operations  13.5 us (7%)
  matrix products  8.14 us (4%)
  other arithmetic  8.02 us (4%)
  local copies, waits for them, and re-layouts  2.87 us (2%)
    all_gather x1, waiting for transfers between devices, on_device(): lax.all_gather(matrix, 'col', axis=1, tiled=True)  83.7 us
    all_gather x1, waiting for transfers between devices, on_device(): col_panel = lax.all_gather(matrix, 'row', axis=0, tiled=True)  53.6 us
    psum x1, blocking collectives, on_device(): col_means = lax.psum(jnp.sum(part_prod, axis=0), 'row') / order_all  9.85 us
    dot_general x1, matrix products, on_device(): jnp.dot(lax.all_gather(matrix, 'col', axis=1, tiled=True), col_panel, pre...  8.14 us
    psum x1, blocking collectives, on_device(): col_totals = lax.psum(jnp.sum(pruned, axis=0), 'row') / order_all  7.98 us
  transfers between devices with their start and end apart: 2, of which 2 were waited for; matrix products, arithmetic and copies ran while one was open for 0% of the time, Pallas kernels for 0%

commit v1 on v0

--- a/solution.py
+++ b/solution.py
@@ -19,7 +19,12 @@
     ).reshape(row_count, col_count)
     order_all = row_count * lax.axis_size("row")
     thresholds = 0.125 * thr_index.astype(jnp.float32)
-    col_panel = lax.all_gather(matrix, "row", axis=0, tiled=True)
+    ring = [matrix]
+    for hop in range(3):
+        ring.append(lax.ppermute(ring[-1], "row", [(dev, (dev + 1) % 4) for dev in range(4)]))
+    col_panel = jnp.roll(
+        jnp.concatenate(ring[::-1], axis=0), (lax.axis_index("row") + 1) * ring[0].shape[0], axis=0
+    )
     product = jnp.dot(
         lax.all_gather(matrix, "col", axis=1, tiled=True),
         col_panel,

time: 189 us -> 143 us (0.76)
  waiting for transfers between devices: 138 us -> 72.4 us
  local copies, waits for them, and re-layouts: 2.87 us -> 18.1 us
  starting transfers between devices: 0.04 us -> 3.81 us
    all_gather x1, waiting for transfers between devices: 83.7 us -> 0.01 us  [on_device(): lax.all_gather(matrix, 'col', axis=1, tiled=True)]
    ppermute x0 -> x3, waiting for transfers between devices: none -> 72.4 us  [on_device(): lax.ppermute(ring[-1], 'row', [(dev, (dev + 1) % 4) for dev in range(4)])]
    all_gather x1 -> x0, waiting for transfers between devices: 53.6 us -> none  [on_device(): col_panel = lax.all_gather(matrix, 'row', axis=0, tiled=True)]
    unnamed x7 -> x18, local copies, waits for them, and re-layouts: 2.02 us -> 16.2 us
    ppermute x0 -> x3, starting transfers between devices: none -> 3.81 us  [on_device(): lax.ppermute(ring[-1], 'row', [(dev, (dev + 1) % 4) for dev in range(4)])]
    psum x1, blocking collectives: 9.85 us -> 7.47 us  [on_device(): col_means = lax.psum(jnp.sum(part_prod, axis=0), 'row') / order_all]
    psum x1, blocking collectives: 7.98 us -> 9.99 us  [on_device(): col_totals = lax.psum(jnp.sum(pruned, axis=0), 'row') / order_all]
  transfers between devices with their start and end apart: 2 -> 4, of which waited for: 2 -> 3; matrix products, arithmetic and copies ran while one was open for 0% -> 11% of each run, Pallas kernels for 0% -> 0%
where the time goes in v1:
time: 143 us; the launch traced here: 142 us
  waiting for transfers between devices  72.4 us (51%)
  local copies, waits for them, and re-layouts  18.1 us (13%)
  blocking collectives  17.5 us (12%)
  between operations  13.5 us (9%)
  other arithmetic  8.71 us (6%)
  matrix products  8.14 us (6%)
  starting transfers between devices  3.81 us (3%)
    ppermute x3, waiting for transfers between devices, on_device(): lax.ppermute(ring[-1], 'row', [(dev, (dev + 1) % 4) for dev in range(4)])  72.4 us
    unnamed x18, local copies, waits for them, and re-layouts  16.2 us
    psum x1, blocking collectives, on_device(): col_totals = lax.psum(jnp.sum(pruned, axis=0), 'row') / order_all  9.99 us
    dot_general x1, matrix products, on_device(): jnp.dot(lax.all_gather(matrix, 'col', axis=1, tiled=True), col_panel, pre...  8.14 us
    psum x1, blocking collectives, on_device(): col_means = lax.psum(jnp.sum(part_prod, axis=0), 'row') / order_all  7.47 us
    ppermute x3, starting transfers between devices, on_device(): lax.ppermute(ring[-1], 'row', [(dev, (dev + 1) % 4) for dev in range(4)])  3.81 us
  transfers between devices with their start and end apart: 4, of which 3 were waited for; matrix products, arithmetic and copies ran while one was open for 11% of the time, Pallas kernels for 0%

profile of v1, /device:TPU:0, one launch (start us, length us, event | category | flops | bytes accessed | tf_op | source)
XLA Modules:
  0.0 142.1 jit_solution(16810162328017821033)
XLA Ops:
  6.5 0.0 copy-start.4
  6.5 0.0 all-gather.2.cloned.1.call-start
  6.5 0.7 convert_element_type.12
  7.2 0.1 copy.5
  7.3 0.3 mul.44
  7.7 2.3 %bitcast_multiply_fusion = bf16[1024,512]{1,0:T(8,128)(2,1)} fusion(bf16[1024,512]{1,0:T(8,128)(2,1)} %param.4, bf16[128,8,4,128]{3,2,1,0:T(4,128)(2,1)S(1)} %bitcast.13), kind=kLoop, calls=%fused_computation.3 | loop fusion | flops 524288 | bytes 3145728 | tf_op jit(solution)/shard_map/mul | solution.py:14
  10.0 0.0 copy-start.1
  10.0 0.0 all-gather.2.cloned.1.call-update
  10.0 3.0 %collective-permute-start = (bf16[1024,512]{1,0:T(8,128)(2,1)}, bf16[1024,512]{1,0:T(8,128)(2,1)S(1)}, u32[]{:S(2)}, u32[]{:S(2)}) collective-permute-start(bf16[1024,512]{1,0:T(8,128)(2,1)} %bitcast_multiply_fusion), channel_id=1, source_target_pairs={{0,8},{8,16},{16,24},{24,0},{1,9},{9,17},{17,25},{25,1},{2,10},{10... | collective-permute-start | bytes 3145736 | tf_op jit(solution)/shard_map/ppermute | solution.py:24
  13.1 24.3 %collective-permute-done = bf16[1024,512]{1,0:T(8,128)(2,1)S(1)} collective-permute-done((bf16[1024,512]{1,0:T(8,128)(2,1)}, bf16[1024,512]{1,0:T(8,128)(2,1)S(1)}, u32[]{:S(2)}, u32[]{:S(2)}) %collective-permute-start) | collective-permute-done | bytes 1048608 | tf_op jit(solution)/shard_map/ppermute | solution.py:24
  37.4 0.0 copy-start.2
  37.4 1.0 copy-done.2
  38.4 0.8 collective-permute-start.1
  39.2 24.6 %collective-permute-done.1 = bf16[1024,512]{1,0:T(8,128)(2,1)} collective-permute-done((bf16[1024,512]{1,0:T(8,128)(2,1)S(1)}, bf16[1024,512]{1,0:T(8,128)(2,1)}, u32[]{:S(2)}, u32[]{:S(2)}) %collective-permute-start.1) | collective-permute-done | bytes 1048608 | tf_op jit(solution)/shard_map/ppermute | solution.py:24
  63.8 0.0 collective-permute-start.2
  63.8 0.7 convert_element_type.14
  64.5 0.1 copy.6
  64.6 0.3 broadcast_in_dim.2
  64.9 0.2 copy.11
  65.1 0.0 copy-done.4
  65.1 0.0 copy-start.3
  65.2 23.5 %collective-permute-done.2 = bf16[1024,512]{1,0:T(8,128)(2,1)} collective-permute-done((bf16[1024,512]{1,0:T(8,128)(2,1)}, bf16[1024,512]{1,0:T(8,128)(2,1)}, u32[]{:S(2)}, u32[]{:S(2)}) %collective-permute-start.2) | collective-permute-done | bytes 1048608 | tf_op jit(solution)/shard_map/ppermute | solution.py:24
  88.6 2.4 %constant_dynamic-update-slice_fusion.7 = bf16[8192,512]{1,0:T(8,128)(2,1)} fusion(bf16[1024,512]{1,0:T(8,128)(2,1)} %collective-permute-done.2), kind=kLoop, calls=%fused_computation.28 | loop fusion | bytes 2097152
  91.0 2.3 %constant_dynamic-update-slice_fusion.6 = bf16[8192,512]{1,0:T(8,128)(2,1)} fusion(bf16[8192,512]{1,0:T(8,128)(2,1)} %constant_dynamic-update-slice_fusion.7, bf16[1024,512]{1,0:T(8,128)(2,1)} %collective-permute-done.1), kind=kLoop, calls=%fused_computation.27 | loop fusion | bytes 2097152
  93.3 2.3 %constant_dynamic-update-slice_fusion.5 = bf16[8192,512]{1,0:T(8,128)(2,1)} fusion(bf16[8192,512]{1,0:T(8,128)(2,1)} %constant_dynamic-update-slice_fusion.6, bf16[1024,512]{1,0:T(8,128)(2,1)} %copy-done.2), kind=kLoop, calls=%fused_computation.26 | loop fusion | bytes 2097152
  95.5 0.0 copy-done.1
  95.6 1.0 constant_dynamic-update-slice_fusion.4
  96.6 2.3 %constant_dynamic-update-slice_fusion.3 = bf16[8192,512]{1,0:T(8,128)(2,1)} fusion(bf16[8192,512]{1,0:T(8,128)(2,1)} %constant_dynamic-update-slice_fusion.4, bf16[1024,512]{1,0:T(8,128)(2,1)} %collective-permute-done.2), kind=kLoop, calls=%fused_computation.24 | loop fusion | bytes 2097152
  98.9 2.3 %constant_dynamic-update-slice_fusion.2 = bf16[8192,512]{1,0:T(8,128)(2,1)} fusion(bf16[8192,512]{1,0:T(8,128)(2,1)} %constant_dynamic-update-slice_fusion.3, bf16[1024,512]{1,0:T(8,128)(2,1)} %collective-permute-done.1), kind=kLoop, calls=%fused_computation.23 | loop fusion | bytes 2097152
  101.2 0.0 copy-done.3
  101.2 1.0 constant_dynamic-update-slice_fusion.1
  102.2 1.1 constant_dynamic-update-slice_fusion
  103.3 0.0 all-gather.2.cloned.1.call-done
  103.3 8.1 %fusion = f32[1024,512]{1,0:T(8,128)S(1)} fusion(bf16[1024,4096]{1,0:T(8,128)(2,1)} %all-gather.2.cloned.1.call-done, bf16[8192,512]{1,0:T(8,128)(2,1)} %constant_dynamic-update-slice_fusion, s32[]{:T(128)S(6)} %select_n.14), kind=kOutput, calls=%fused_computation | convolution fusion | flops 4294967296 | bytes 14680068 | tf_op jit(solution)/shard_map/dot_general | solution.py:28
  111.5 0.0 copy-start
  111.5 1.3 copy-done
  112.8 0.2 slice_reduce_fusion.3
  113.0 7.5 %all-reduce.1 = (f32[128]{0:T(128)S(1)}, f32[128]{0:T(128)S(1)}, f32[128]{0:T(128)S(1)}, f32[128]{0:T(128)S(1)}) all-reduce(f32[128]{0:T(128)S(1)} %get-tuple-element.9, f32[128]{0:T(128)S(1)} %get-tuple-element.10, f32[128]{0:T(128)S(1)} %get-tuple-element.11, f32[128]{0:T(128)S(1)} %get-tuple-element.12), channel_id=1, replica_groups=mesh['row'=4,'col'=8] {'row'}, use_global_device_ids=true, to_apply=%region_1.2 | all-reduce | flops 512 | bytes 4096 | tf_op jit(solution)/shard_map/psum | solution.py:37
  120.4 1.8 %fusion.2 = (f32[128]{0:T(128)S(1)}, f32[128]{0:T(128)S(1)}, f32[128]{0:T(128)S(1)}, f32[128]{0:T(128)S(1)}) fusion(f32[1024,512]{1,0:T(8,128)S(1)} %bitcast.10, f32[128]{0:T(128)S(1)} %get-tuple-element.28, f32[1024,512]{1,0:T(8,128)} %copy-done, f32[128]{0:T(128)S(1)} %get-tuple-element.26, f32[128]{0:T(128)S(1)} %get-tuple-element.27, ...), kind=kLoop, calls=%fused_computation.17 | loop fusion | flops 2096640 | bytes 4198400 | tf_op jit(solution)/shard_map/reduce_sum | solution.py:42
  122.3 10.0 %all-reduce = (f32[128]{0:T(128)S(1)}, f32[128]{0:T(128)S(1)}, f32[128]{0:T(128)S(1)}, f32[128]{0:T(128)S(1)}) all-reduce(f32[128]{0:T(128)S(1)} %get-tuple-element.6, f32[128]{0:T(128)S(1)} %get-tuple-element.7, f32[128]{0:T(128)S(1)} %get-tuple-element.8, f32[128]{0:T(128)S(1)} %get-tuple-element.5), channel_id=1, replica_groups=mesh['row'=4,'col'=8] {'row'}, use_global_device_ids=true, to_apply=%region_15.16 | all-reduce | flops 512 | bytes 4096 | tf_op jit(solution)/shard_map/psum | solution.py:42
  132.3 1.9 %divide_convert_fusion.3 = (bf16[1024,128]{1,0:T(8,128)(2,1)S(1)}, bf16[1024,128]{1,0:T(8,128)(2,1)S(1)}, bf16[1024,128]{1,0:T(8,128)(2,1)S(1)}, bf16[1024,128]{1,0:T(8,128)(2,1)S(1)}) fusion(f32[128]{0:T(128)S(1)} %get-tuple-element.32, f32[1024,512]{1,0:T(8,128)S(1)} %bitcast.11, f32[128]{0:T(128)S(1)} %get-tuple-element.28, f32[1024,512]{1,0:T(8,128)} %copy-done, ...), kind=kLoop, calls=%fused_computation.12 | loop fusion | flops 2621440 | bytes 5246976 | tf_op jit(solution)/shard_map/convert
  134.2 1.1 pad_maximum_fusion
  (4 shorter events, 0.0 us)
Async XLA Ops:
  6.5 58.6 %copy-start.4 = (s32[512]{0:T(512)S(1)}, s32[512]{0:T(512)}, u32[]{:S(2)}) copy-start(s32[512]{0:T(512)} %param.7) | copy-start | bytes 6148
  6.5 96.8 %all-gather.2.cloned.1.call-start = ((), (), s32[]{:S(2)}) async-start(), calls=%async_computation | async-start | bytes 9437184 | tf_op jit(solution)/shard_map/all_gather | solution.py:29
  10.0 85.5 %copy-start.1 = (bf16[1024,512]{1,0:T(8,128)(2,1)S(1)}, bf16[1024,512]{1,0:T(8,128)(2,1)}, u32[]{:S(2)}) copy-start(bf16[1024,512]{1,0:T(8,128)(2,1)} %bitcast_multiply_fusion) | copy-start | bytes 3145732
  10.0 27.3 %collective-permute-start = (bf16[1024,512]{1,0:T(8,128)(2,1)}, bf16[1024,512]{1,0:T(8,128)(2,1)S(1)}, u32[]{:S(2)}, u32[]{:S(2)}) collective-permute-start(bf16[1024,512]{1,0:T(8,128)(2,1)} %bitcast_multiply_fusion), channel_id=1, source_target_pairs={{0,8},{8,16},{16,24},{24,0},{1,9},{9,17},{17,25},{25,1},{2,10},{10... | collective-permute-start | bytes 3145736 | tf_op jit(solution)/shard_map/ppermute | solution.py:24
  37.4 1.0 copy-start.2
  38.4 25.4 %collective-permute-start.1 = (bf16[1024,512]{1,0:T(8,128)(2,1)S(1)}, bf16[1024,512]{1,0:T(8,128)(2,1)}, u32[]{:S(2)}, u32[]{:S(2)}) collective-permute-start(bf16[1024,512]{1,0:T(8,128)(2,1)S(1)} %collective-permute-done), channel_id=1, source_target_pairs={{0,8},{8,16},{16,24},{24,0},{1,9},{9,17},{17,25},{25,1},{2,10},{10... | collective-permute-start | bytes 3145736 | tf_op jit(solution)/shard_map/ppermute | solution.py:24
  63.8 24.8 %collective-permute-start.2 = (bf16[1024,512]{1,0:T(8,128)(2,1)}, bf16[1024,512]{1,0:T(8,128)(2,1)}, u32[]{:S(2)}, u32[]{:S(2)}) collective-permute-start(bf16[1024,512]{1,0:T(8,128)(2,1)} %collective-permute-done.1), channel_id=1, source_target_pairs={{0,8},{8,16},{16,24},{24,0},{1,9},{9,17},{17,25},{25,1},{2,10},{10... | collective-permute-start | bytes 3145736 | tf_op jit(solution)/shard_map/ppermute | solution.py:24
  65.1 36.1 %copy-start.3 = (bf16[1024,512]{1,0:T(8,128)(2,1)S(1)}, bf16[1024,512]{1,0:T(8,128)(2,1)}, u32[]{:S(2)}) copy-start(bf16[1024,512]{1,0:T(8,128)(2,1)} %copy-done.2) | copy-start | bytes 3145732
  111.5 1.4 copy-start
Sparse Core Ops, SparseCore 0:
  10.2 84.7 all-gather.1
